TPU v7x, 32 devices: a whole 2x2x4 slice. The times are simulated.
32 devices in a mesh: gx: 4 (over z), gy: 4 (over y, core), gz: 2 (over x).
Axes of the slice: x: 2, y: 2, z: 4, core: 2. Of those that a mesh axis runs over, the one named last changes fastest.
Arguments:
- gradients: bfloat16 [32, 768, 512], P(('gx', 'gy', 'gz')), may hold values from -6 to 6
- master_weights: float32 [768, 512], P(('gx', 'gy', 'gz')), may hold values from -10 to 10
- first_moment: float32 [768, 512], P(('gx', 'gy', 'gz')), may hold values from -8 to 8
- second_moment: float32 [768, 512], P(('gx', 'gy', 'gz')), may hold values from 1 to 100
- tensor_ids: int32 [768], P(('gx', 'gy', 'gz')), may hold values from 0 to 3, as said below
Outputs:
- new_master: float32 [768, 512], P(('gx', 'gy', 'gz'))
- new_first: float32 [768, 512], P(('gx', 'gy', 'gz'))
- new_second: float32 [768, 512], P(('gx', 'gy', 'gz'))
- scaled_update: float32 [768, 512], P(('gx', 'gy', 'gz'))
- params: bfloat16 [768, 512], replicated
Inputs may be any that keep to these rules, and one draw needn't show every extreme that they name: `tensor_ids`: nondecreasing along the rows; every tensor of 4 owns one contiguous run of rows.
All inputs are finite; a program needn't handle non-finite values.
Results may differ from a plain program's by a relative error of at most 0.0045.
Values may be sent and summed in bfloat16 or wider, within the bound.
A program may use at most 64 MiB of HBM per device.

v0:
```python
import jax
import jax.numpy as jnp
from jax import lax
from jax.sharding import PartitionSpec as P

NT = 4


decay_first = 0.9
decay_second = 0.999
epsilon = 1e-06
weight_decay = 0.01
step_size = 0.05


def tensor_sums(values, onehot):
    return jnp.dot(jnp.sum(values * values, axis=1), onehot, precision=lax.Precision.HIGHEST)


def on_device(gradients, master_weights, first_moment, second_moment, tensor_ids):
    count_across = lax.axis_size("gx")
    count_down = lax.axis_size("gy")
    count_along = lax.axis_size("gz")
    own_rows, row_width = master_weights.shape
    own_gradient = gradients[0].astype(jnp.float32)
    onehot = (tensor_ids[:, None] == jnp.arange(NT, dtype=jnp.int32)[None, :]).astype(jnp.float32)
    counts = jnp.sum(onehot, axis=0) * row_width
    weight_local = tensor_sums(master_weights, onehot)
    summed = lax.psum_scatter(own_gradient, ("gx", "gy", "gz"), scatter_dimension=0, tiled=True)
    new_first = decay_first * first_moment + (1.0 - decay_first) * summed
    new_second = decay_second * second_moment + (1.0 - decay_second) * summed * summed
    update = new_first / (jnp.sqrt(new_second) + epsilon) + weight_decay * master_weights
    update_local = tensor_sums(update, onehot)
    weight_sq, update_sq, total_counts = lax.psum(
        (weight_local, update_local, counts), ("gx", "gy", "gz")
    )
    trust_ratio = jnp.sqrt(weight_sq / (update_sq + total_counts))
    row_trust = jnp.dot(onehot, trust_ratio, precision=lax.Precision.HIGHEST)
    scaled_update = row_trust[:, None] * update
    new_master = master_weights - step_size * scaled_update
    params = new_master.astype(jnp.bfloat16)
    stacked = params.reshape(1, 1, 1, own_rows, row_width)
    stacked = lax.all_gather(stacked, "gz", axis=2, tiled=True)
    stacked = lax.all_gather(stacked, "gy", axis=1, tiled=True)
    stacked = lax.all_gather(stacked, "gx", axis=0, tiled=True)
    gathered = stacked.reshape(count_across * count_down * count_along * own_rows, row_width)
    return (new_master, new_first, new_second, scaled_update, gathered)


def solution(mesh):
    placed = (
        P(("gx", "gy", "gz"), None, None),
        P(("gx", "gy", "gz"), None),
        P(("gx", "gy", "gz"), None),
        P(("gx", "gy", "gz"), None),
        P(("gx", "gy", "gz")),
    )
    return jax.shard_map(
        on_device,
        mesh=mesh,
        in_specs=placed,
        out_specs=(
            P(("gx", "gy", "gz"), None),
            P(("gx", "gy", "gz"), None),
            P(("gx", "gy", "gz"), None),
            P(("gx", "gy", "gz"), None),
            P(),
        ),
        check_vma=False,
    )
```

profile of v0, /device:TPU:0, one launch (start us, length us, event | category | flops | bytes accessed | tf_op | source)
XLA Modules:
  0.0 192.9 jit_solution(224679185084797779)
XLA Ops:
  7.2 0.0 copy-start.3
  7.2 0.0 copy-start
  7.2 0.0 copy-start.1
  7.2 0.0 copy-start.2
  7.2 0.0 reduce-scatter.2.cloned.1.call-start
  7.3 2.5 %bitcast_convert_fusion = f32[768,512]{1,0:T(8,128)} fusion(bf16[1,768,512]{2,1,0:T(8,128)(2,1)} %param.5), kind=kLoop, calls=%fused_computation.4 | loop fusion | flops 393216 | bytes 2359296 | tf_op jit(solution)/shard_map/convert_element_type | solution.py:25
  9.8 0.0 reduce-scatter.2.cloned.1.call-update
  9.8 0.0 copy-done.3
  9.8 0.1 convert_reduce_fusion
  9.9 104.0 %reduce-scatter.2.cloned.1.call-done = f32[24,512]{1,0:T(8,128)} async-done(((f32[768,512]{1,0:T(8,128)}), f32[24,512]{1,0:T(8,128)}) %reduce-scatter.2.cloned.1.call-update) | async-done | bytes 49168 | tf_op jit(solution)/shard_map/reduce_scatter | solution.py:29
  113.9 0.0 copy-done
  113.9 0.0 copy-done.1
  113.9 0.0 copy-done.2
  113.9 1.6 multiply_reduce_fusion
  115.5 0.1 fusion
  115.6 0.1 convolution_bitcast_fusion.2
  115.7 40.1 %all-reduce = (f32[4]{0:T(128)S(1)}, f32[4]{0:T(128)S(1)}) all-reduce(f32[4]{0:T(128)S(1)} %convolution_bitcast_fusion.2, f32[4]{0:T(128)S(1)} %fusion), channel_id=1, replica_groups=mesh['gx'=4,'gy'=4,'gz'=2] {'gx','gy','gz'}, use_global_device_ids=true, to_apply=%region_1.0 | all-reduce | flops 8 | bytes 64 | tf_op jit(solution)/shard_map/psum | solution.py:34
  155.8 0.1 convolution_bitcast_fusion
  155.9 0.7 fusion.8
  156.6 4.7 %all-gather = bf16[48,512]{1,0:T(8,128)(2,1)S(1)} all-gather(bf16[24,512]{1,0:T(8,128)(2,1)S(1)} %get-tuple-element.7), channel_id=2, replica_groups=mesh['gx'=4,'gy'=4,'gz'=2] {'gz'}, dimensions={0}, use_global_device_ids=true | all-gather | bytes 73728 | tf_op jit(solution)/shard_map/all_gather | solution.py:43
  161.4 5.9 %all_gather.10 = bf16[1,4,2,24,512]{4,3,2,0,1:T(8,128)(2,1)S(1)} all-gather(bf16[1,1,2,24,512]{4,3,2,0,1:T(8,128)(2,1)S(1)} %bitcast.25), channel_id=1, replica_groups=mesh['gx'=4,'gy'=4,'gz'=2] {'gy'}, dimensions={1}, use_global_device_ids=true | all-gather | bytes 245760 | tf_op jit(solution)/shard_map/all_gather | solution.py:44
  167.3 17.9 %all_gather.11 = bf16[4,4,2,24,512]{4,3,2,1,0:T(8,128)(2,1)S(1)} all-gather(bf16[1,4,2,24,512]{4,3,2,1,0:T(8,128)(2,1)S(1)} %bitcast.24), channel_id=1, replica_groups=mesh['gx'=4,'gy'=4,'gz'=2] {'gx'}, dimensions={0}, use_global_device_ids=true | all-gather | bytes 983040 | tf_op jit(solution)/shard_map/all_gather | solution.py:45
  185.2 0.9 copy.13
Async XLA Ops:
  7.2 2.6 %copy-start.3 = (s32[24]{0:T(128)S(1)}, s32[24]{0:T(128)}, u32[]{:S(2)}) copy-start(s32[24]{0:T(128)} %param.9) | copy-start | bytes 292
  7.2 106.7 %copy-start = (f32[24,512]{1,0:T(8,128)S(1)}, f32[24,512]{1,0:T(8,128)}, u32[]{:S(2)}) copy-start(f32[24,512]{1,0:T(8,128)} %param.6) | copy-start | bytes 147460
  7.2 106.7 %copy-start.1 = (f32[24,512]{1,0:T(8,128)S(1)}, f32[24,512]{1,0:T(8,128)}, u32[]{:S(2)}) copy-start(f32[24,512]{1,0:T(8,128)} %param.8) | copy-start | bytes 147460
  7.2 106.7 %copy-start.2 = (f32[24,512]{1,0:T(8,128)S(1)}, f32[24,512]{1,0:T(8,128)}, u32[]{:S(2)}) copy-start(f32[24,512]{1,0:T(8,128)} %param.7) | copy-start | bytes 147460
  7.2 106.7 %reduce-scatter.2.cloned.1.call-start = ((), (), s32[]{:S(2)}) async-start(), calls=%async_computation.1 | async-start | bytes 1622016 | tf_op jit(solution)/shard_map/reduce_scatter | solution.py:29
Sparse Core Ops, SparseCore 0:
  13.3 100.5 reduce-scatter.1
where the time goes:
time: 193 us
  waiting for transfers between devices  104 us (54%)
  blocking collectives  68.6 us (36%)
  between operations  14.1 us (7%)
  other arithmetic  4.92 us (3%)
    reduce_scatter x1, waiting for transfers between devices, on_device(): lax.psum_scatter(own_gradient, ('gx', 'gy', 'gz'), scatter_dimension=0, t...  104 us
    psum x1, blocking collectives, on_device(): lax.psum((weight_local, update_local, counts), ('gx', 'gy', 'gz'))  40.1 us
    all_gather x1, blocking collectives, on_device(): stacked = lax.all_gather(stacked, 'gx', axis=0, tiled=True)  17.9 us
    all_gather x1, blocking collectives, on_device(): stacked = lax.all_gather(stacked, 'gy', axis=1, tiled=True)  5.92 us
    all_gather x1, blocking collectives, on_device(): stacked = lax.all_gather(stacked, 'gz', axis=2, tiled=True)  4.72 us
  transfers between devices with their start and end apart: 1, of which 1 were waited for; matrix products, arithmetic and copies ran while one was open for 0% of the time, Pallas kernels for 0%

commit v1 on v0

v1 whole, which is shorter than its diff:
```python
import functools
import itertools

import jax
import jax.numpy as jnp
from jax import lax
from jax.experimental import pallas as pl
from jax.experimental.pallas import tpu as pltpu
from jax.sharding import PartitionSpec as P

NT = 4
MESH = pl.DeviceIdType.MESH

decay_first = 0.9
decay_second = 0.999
epsilon = 1e-06
weight_decay = 0.01
step_size = 0.05


def digits_of(extent):
    factors, base = [], 2
    while extent > 1:
        while extent % base == 0:
            factors.append(base)
            extent //= base
        base += 1
    return factors


def offset(index, amount, extent, sign=1):
    result, weight = 0, 1
    for base in digits_of(extent):
        step = (amount // weight) % base
        digit = index if weight == 1 else index // weight
        if weight * base < extent:
            digit = digit % base
        if step:
            digit = (digit + (step if sign > 0 else base - step)) % base
        result = result + weight * digit
        weight *= base
    return result


def kernel(
    sizes, grads, master, first, second, ids,
    out_master, out_first, out_second, out_scaled, out_params,
    own_half, far_half, pair_recv, pair_send, plane_recv, line_send, line_recv, acc,
    m_in, f_in, s_in, m_out, u_out, sums_send, sums_recv, gathered,
    load_own, load_far, load_small, pair_ss, pair_rs, plane_ss, plane_rs, line_ss, line_rs,
    sums_ss, sums_rs, gl_ss, gl_rs, gp_ss, gp_rs, gs_ss, gs_rs, store_sem, small_sem,
):
    A, Y, S, X = sizes
    rows, width = master.shape
    a = lax.axis_index("gx")
    gy = lax.axis_index("gy")
    x = lax.axis_index("gz")
    y, c = gy // S, gy % S

    def device(a_, y_, c_, x_):
        return (a_, y_ * S + c_, x_)

    def remote(src, dst, ss, rs, where):
        return pltpu.make_async_remote_copy(
            src_ref=src, dst_ref=dst, send_sem=ss, recv_sem=rs, device_id=device(*where), device_id_type=MESH
        )

    plane = [q for q in itertools.product(range(Y), range(X)) if q != (0, 0)]
    lines_far = list(range(A - 1, 0, -1))
    lines_near = list(range(1, A))
    others = [o for o in itertools.product(range(A), range(Y), range(S), range(X)) if o != (0, 0, 0, 0)]

    def at(da, dy, dc, dx, sign=1):
        return (offset(a, da, A, sign), offset(y, dy, Y, sign), offset(c, dc, S, sign), offset(x, dx, X, sign))

    barrier = pltpu.get_barrier_semaphore()
    for o in others:
        pl.semaphore_signal(barrier, inc=1, device_id=device(*at(*o)), device_id_type=MESH)

    loads_own, loads_far = {}, {}
    order = lines_far + [0]
    for d in order:
        target = offset(a, d, A)
        for k in range(1, S):
            loads_far[d, k] = pltpu.make_async_copy(
                grads.at[target, :, offset(c, k, S)], far_half.at[k - 1, d], load_far.at[k - 1, d]
            )
            loads_far[d, k].start()
    for d in order:
        target = offset(a, d, A)
        loads_own[d] = pltpu.make_async_copy(grads.at[target, :, c], own_half.at[d], load_own.at[d])
        loads_own[d].start()
    loads_small = [
        pltpu.make_async_copy(src, dst, load_small.at[i])
        for i, (src, dst) in enumerate(((master, m_in), (first, f_in), (second, s_in)))
    ]
    for copy in loads_small:
        copy.start()

    pl.semaphore_wait(barrier, len(others))

    sends = []
    pair = {}
    for d in order:
        for k in range(1, S):
            loads_far[d, k].wait()
            pair[d, k] = remote(
                far_half.at[k - 1, d], pair_recv.at[k - 1, d], pair_ss.at[k - 1, d], pair_rs.at[k - 1, d], at(0, 0, k, 0)
            )
            pair[d, k].start()

    ids_row = jnp.broadcast_to(ids[...], (rows, rows)).astype(jnp.float32)
    diagonal = lax.broadcasted_iota(jnp.int32, (rows, rows), 0) == lax.broadcasted_iota(jnp.int32, (rows, rows), 1)
    ids_col = jnp.sum(jnp.where(diagonal, ids_row, 0.0), axis=1, keepdims=True)
    lane = lax.broadcasted_iota(jnp.int32, (rows, 128), 1).astype(jnp.float32)
    hit_w, hit_u, hit_n = lane == ids_col, lane == ids_col + NT, lane == ids_col + 2 * NT
    for copy in loads_small:
        copy.wait()
    weights = m_in[...]
    weight_rows = jnp.sum(weights * weights, axis=1, keepdims=True)
    fixed_sums = jnp.where(hit_w, weight_rows, 0.0) + jnp.where(hit_n, float(width), 0.0)

    crossing = {}
    for d in order:
        loads_own[d].wait()
        for k in range(1, S):
            pair[d, k].wait_recv()
        for i, (dy, dx) in enumerate(plane):
            y_, x_ = offset(y, dy, Y), offset(x, dx, X)
            total = own_half[d, y_, x_].astype(jnp.float32)
            for k in range(1, S):
                total = total + pair_recv[k - 1, d, y_, x_].astype(jnp.float32)
            pair_send[d, i] = total.astype(jnp.bfloat16)
            crossing[d, i] = remote(
                pair_send.at[d, i], plane_recv.at[d, i], plane_ss.at[d, i], plane_rs.at[d, i], at(0, dy, 0, dx)
            )
            crossing[d, i].start()
        total = own_half[d, y, x].astype(jnp.float32)
        for k in range(1, S):
            total = total + pair_recv[k - 1, d, y, x].astype(jnp.float32)
        acc[d] = total

    along = {}
    for d in order:
        total = acc[d]
        for i in range(len(plane)):
            crossing[d, i].wait_recv()
            total = total + plane_recv[d, i].astype(jnp.float32)
        if d:
            line_send[d - 1] = total.astype(jnp.bfloat16)
            along[d] = remote(
                line_send.at[d - 1], line_recv.at[d - 1], line_ss.at[d - 1], line_rs.at[d - 1], at(d, 0, 0, 0)
            )
            along[d].start()
    summed = total
    for d in lines_near:
        along[d].wait_recv()
        summed = summed + line_recv[d - 1].astype(jnp.float32)

    new_first = decay_first * f_in[...] + (1.0 - decay_first) * summed
    new_second = decay_second * s_in[...] + (1.0 - decay_second) * summed * summed
    update = new_first / (jnp.sqrt(new_second) + epsilon) + weight_decay * weights
    update_rows = jnp.sum(update * update, axis=1, keepdims=True)
    own_sums = jnp.sum(fixed_sums + jnp.where(hit_u, update_rows, 0.0), axis=0, keepdims=True)
    sums_send[...] = own_sums
    exchange = []
    for i, o in enumerate(reversed(others)):
        exchange.append(remote(sums_send, sums_recv.at[i], sums_ss.at[i], sums_rs.at[i], at(*o)))
        exchange[-1].start()
    f_in[...] = new_first
    s_in[...] = new_second
    smalls = [
        pltpu.make_async_copy(f_in, out_first, small_sem.at[0]),
        pltpu.make_async_copy(s_in, out_second, small_sem.at[1]),
    ]
    for copy in smalls:
        copy.start()
    totals = own_sums
    for i in reversed(range(len(others))):
        exchange[i].wait_recv()
        totals = totals + sums_recv[i]
    row_totals = jnp.broadcast_to(totals, (rows, 128))
    row_weight, row_update, row_count = (
        jnp.sum(jnp.where(hit, row_totals, 0.0), axis=1, keepdims=True) for hit in (hit_w, hit_u, hit_n)
    )
    trust = jnp.sqrt(row_weight / (row_update + row_count))
    scaled = trust * update
    new_master = weights - step_size * scaled
    gathered[a, y, c, x] = new_master.astype(jnp.bfloat16)

    stores = []

    def store(where, slot):
        copy = pltpu.make_async_copy(gathered.at[where], out_params.at[where], store_sem.at[slot])
        copy.start()
        stores.append(copy)

    slots = iter(range(A * Y * S * X))
    own = (a, y, c, x)
    line_hops, plane_hops, core_hops = {}, {}, {}
    for d in lines_far:
        line_hops[d] = remote(gathered.at[own], gathered.at[own], gl_ss.at[d - 1], gl_rs.at[d - 1], at(d, 0, 0, 0))
        line_hops[d].start()

    def to_plane(d):
        block = at(d, 0, 0, 0, -1)
        for i, (dy, dx) in enumerate(plane):
            plane_hops[d, i] = remote(
                gathered.at[block], gathered.at[block], gp_ss.at[d, i], gp_rs.at[d, i], at(0, dy, 0, dx)
            )
            plane_hops[d, i].start()

    def to_cores(d, i, block):
        for k in range(1, S):
            core_hops[d, i, k] = remote(
                gathered.at[block], gathered.at[block], gs_ss.at[k - 1, d, i], gs_rs.at[k - 1, d, i], at(0, 0, k, 0)
            )
            core_hops[d, i, k].start()

    to_plane(0)
    to_cores(0, len(plane), own)
    m_out[...] = new_master
    u_out[...] = scaled
    for i, (src, dst) in enumerate(((m_out, out_master), (u_out, out_scaled))):
        smalls.append(pltpu.make_async_copy(src, dst, small_sem.at[2 + i]))
        smalls[-1].start()
    store(own, next(slots))
    for d in lines_near:
        line_hops[d].wait_recv()
        block = at(d, 0, 0, 0, -1)
        to_plane(d)
        to_cores(d, len(plane), block)
        store(block, next(slots))
    for d in [0] + lines_near:
        for i, (dy, dx) in enumerate(plane):
            plane_hops[d, i].wait_recv()
            block = at(d, dy, 0, dx, -1)
            to_cores(d, i, block)
            store(block, next(slots))
    for d in [0] + lines_near:
        for i, (dy, dx) in [(len(plane), (0, 0))] + list(enumerate(plane)):
            for k in range(1, S):
                core_hops[d, i, k].wait_recv()
                store(at(d, dy, k, dx, -1), next(slots))

    for group in (pair, crossing, along, line_hops, plane_hops, core_hops):
        for copy in group.values():
            copy.wait_send()
    for copy in exchange:
        copy.wait_send()
    for copy in stores + smalls:
        copy.wait()


def solution(mesh):
    A, gy, X = mesh.shape["gx"], mesh.shape["gy"], mesh.shape["gz"]
    S = 2 if gy % 2 == 0 else 1
    Y = gy // S
    total = A * gy * X
    planes = max(Y * X - 1, 1)
    lines = max(A - 1, 1)
    cores = max(S - 1, 1)
    bf16, f32 = jnp.bfloat16, jnp.float32
    dma = pltpu.SemaphoreType.DMA

    def on_device(gradients, master_weights, first_moment, second_moment, tensor_ids):
        rows, width = master_weights.shape
        anywhere = pl.BlockSpec(memory_space=pl.ANY)
        vmem = pltpu.VMEM
        small = jax.ShapeDtypeStruct((rows, width), f32)
        outs = pl.pallas_call(
            functools.partial(kernel, (A, Y, S, X)),
            out_shape=(small, small, small, small, jax.ShapeDtypeStruct((A, Y, S, X, rows, width), bf16)),
            in_specs=[anywhere] * 4 + [pl.BlockSpec(memory_space=vmem)],
            out_specs=(anywhere,) * 5,
            scratch_shapes=[
                vmem((A, Y, X, rows, width), bf16),
                vmem((cores, A, Y, X, rows, width), bf16),
                vmem((cores, A, Y, X, rows, width), bf16),
                vmem((A, planes, rows, width), bf16),
                vmem((A, planes, rows, width), bf16),
                vmem((lines, rows, width), bf16),
                vmem((lines, rows, width), bf16),
                vmem((A, rows, width), f32),
                vmem((rows, width), f32),
                vmem((rows, width), f32),
                vmem((rows, width), f32),
                vmem((rows, width), f32),
                vmem((rows, width), f32),
                vmem((1, 128), f32),
                vmem((max(total - 1, 1), 1, 128), f32),
                vmem((A, Y, S, X, rows, width), bf16),
                dma((A,)), dma((cores, A)), dma((3,)),
                dma((cores, A)), dma((cores, A)),
                dma((A, planes)), dma((A, planes)),
                dma((lines,)), dma((lines,)),
                dma((total,)), dma((total,)),
                dma((lines,)), dma((lines,)),
                dma((A, planes)), dma((A, planes)),
                dma((cores, A, planes + 1)), dma((cores, A, planes + 1)),
                dma((total,)), dma((4,)),
            ],
            compiler_params=pltpu.CompilerParams(collective_id=0, has_side_effects=True),
        )(
            gradients.reshape(A, Y, S, X, rows, width),
            master_weights,
            first_moment,
            second_moment,
            tensor_ids[None, :],
        )
        return (*outs[:4], outs[4].reshape(total * rows, width))

    axes = ("gx", "gy", "gz")
    return jax.shard_map(
        on_device,
        mesh=mesh,
        in_specs=(P(axes, None, None), P(axes, None), P(axes, None), P(axes, None), P(axes)),
        out_specs=(P(axes, None), P(axes, None), P(axes, None), P(axes, None), P()),
        check_vma=False,
    )
```

time: 193 us -> 39.1 us (0.20)
  waiting for transfers between devices: 104 us -> 0 us
  blocking collectives: 68.6 us -> 0 us
  Pallas kernels: 0 us -> 32 us
  between operations: 14.1 us -> 0.65 us
  other arithmetic: 4.92 us -> 0 us
  local copies, waits for them, and re-layouts: 0.9 us -> 5.75 us
    reduce_scatter x1 -> x0, waiting for transfers between devices: 104 us -> none  [on_device(): lax.psum_scatter(own_gradient, ('gx', 'gy', 'gz'), scatter_dimension=0, t...]
    psum x1 -> x0, blocking collectives: 40.1 us -> none  [on_device(): lax.psum((weight_local, update_local, counts), ('gx', 'gy', 'gz'))]
    pallas_call x0 -> x1, Pallas kernels: none -> 32 us  [on_device(): pl.pallas_call(functools.partial(kernel, (A, Y, S, X)), out_shape=(small,...]
    all_gather x3 -> x0, blocking collectives: 28.5 us -> none  [the longest x1 17.9 us: on_device(): stacked = lax.all_gather(stacked, 'gx', axis=0, tiled=True)]
    unnamed x9 -> x11, local copies, waits for them, and re-layouts: 0.9 us -> 5.75 us
    convert_element_type x2 -> x0, other arithmetic: 3.24 us -> none  [the longest x1 2.5 us: on_device(): own_gradient = gradients[0].astype(jnp.float32)]
  transfers between devices with their start and end apart: 1 -> 0, of which waited for: 1 -> 0; matrix products, arithmetic and copies ran while one was open for 0% -> 0% of each run, Pallas kernels for 0% -> 0%
where the time goes in v1:
time: 39.1 us; the launch traced here: 38.4 us
  Pallas kernels  32 us (82%)
  local copies, waits for them, and re-layouts  5.75 us (15%)
  between operations  0.65 us (2%)
    pallas_call x1, Pallas kernels, on_device(): pl.pallas_call(functools.partial(kernel, (A, Y, S, X)), out_shape=(small,...  32 us
    unnamed x11, local copies, waits for them, and re-layouts  5.75 us

profile of v1, /device:TPU:0, one launch (start us, length us, event | category | flops | bytes accessed | tf_op | source)
XLA Modules:
  0.0 38.4 jit_solution(1056447306428333852)
XLA Ops:
  0.6 32.0 %shard_map.92 = (f32[24,512]{1,0:T(8,128)}, f32[24,512]{1,0:T(8,128)}, f32[24,512]{1,0:T(8,128)}, f32[24,512]{1,0:T(8,128)}, bf16[4,2,2,2,24,512]{5,4,3,2,1,0:T(8,128)(2,1)}) custom-call(bf16[4,2,2,2,24,512]{5,4,3,2,1,0:T(8,128)(2,1)} %bitcast.3, f32[24,512]{1,0:T(8,128)} %master.1, f32[24,512]{1,0:T(8,128)} %first.1, f32[24,512]{1,0:T(8,128)} %second.1, ...), custom_call_target="tpu_custom_call" | custom-call | tf_op jit(solution)/shard_map/pallas_call | solution.py:271
  32.6 0.0 copy-start.2
  32.7 1.4 %copy.15 = f32[24,512]{1,0:T(8,128)} copy(f32[24,512]{1,0:T(8,128)} %get-tuple-element.20) | data formatting | bytes 98304
  34.1 0.0 copy-done.2
  34.1 0.0 copy-start.1
  34.1 0.6 %copy.16 = f32[24,512]{1,0:T(8,128)} copy(f32[24,512]{1,0:T(8,128)S(1)} %copy-done.2) | data formatting | bytes 98304
  34.7 0.2 copy-done.1
  34.9 0.0 copy-start
  34.9 0.6 %copy.17 = f32[24,512]{1,0:T(8,128)} copy(f32[24,512]{1,0:T(8,128)S(1)} %copy-done.1) | data formatting | bytes 98304
  35.5 0.2 copy-done
  35.7 0.6 %copy.18 = f32[24,512]{1,0:T(8,128)} copy(f32[24,512]{1,0:T(8,128)S(1)} %copy-done) | data formatting | bytes 98304
  36.3 2.1 %copy.19 = bf16[768,512]{1,0:T(8,128)(2,1)} copy(bf16[768,512]{1,0:T(8,128)(2,1)} %bitcast.4) | data formatting | bytes 1572864
Async XLA Ops:
  32.6 1.4 %copy-start.2 = (f32[24,512]{1,0:T(8,128)S(1)}, f32[24,512]{1,0:T(8,128)}, u32[]{:S(2)}) copy-start(f32[24,512]{1,0:T(8,128)} %get-tuple-element.21) | copy-start | bytes 147460
  34.1 0.8 %copy-start.1 = (f32[24,512]{1,0:T(8,128)S(1)}, f32[24,512]{1,0:T(8,128)}, u32[]{:S(2)}) copy-start(f32[24,512]{1,0:T(8,128)} %get-tuple-element.22) | copy-start | bytes 147460
  34.9 0.8 %copy-start = (f32[24,512]{1,0:T(8,128)S(1)}, f32[24,512]{1,0:T(8,128)}, u32[]{:S(2)}) copy-start(f32[24,512]{1,0:T(8,128)} %get-tuple-element.23) | copy-start | bytes 147460

commit v2 on v1

--- a/solution.py
+++ b/solution.py
@@ -44,11 +44,11 @@
 
 def kernel(
     sizes, grads, master, first, second, ids,
-    out_master, out_first, out_second, out_scaled, out_params,
+    m_out, first_out, second_out, u_out, gathered,
     own_half, far_half, pair_recv, pair_send, plane_recv, line_send, line_recv, acc,
-    m_in, f_in, s_in, m_out, u_out, sums_send, sums_recv, gathered,
+    m_in, f_in, s_in, sums_send, sums_recv,
     load_own, load_far, load_small, pair_ss, pair_rs, plane_ss, plane_rs, line_ss, line_rs,
-    sums_ss, sums_rs, gl_ss, gl_rs, gp_ss, gp_rs, gs_ss, gs_rs, store_sem, small_sem,
+    sums_ss, sums_rs, gl_ss, gl_rs, gp_ss, gp_rs, gs_ss, gs_rs,
 ):
     A, Y, S, X = sizes
     rows, width = master.shape
@@ -167,14 +167,8 @@
     for i, o in enumerate(reversed(others)):
         exchange.append(remote(sums_send, sums_recv.at[i], sums_ss.at[i], sums_rs.at[i], at(*o)))
         exchange[-1].start()
-    f_in[...] = new_first
-    s_in[...] = new_second
-    smalls = [
-        pltpu.make_async_copy(f_in, out_first, small_sem.at[0]),
-        pltpu.make_async_copy(s_in, out_second, small_sem.at[1]),
-    ]
-    for copy in smalls:
-        copy.start()
+    first_out[...] = new_first
+    second_out[...] = new_second
     totals = own_sums
     for i in reversed(range(len(others))):
         exchange[i].wait_recv()
@@ -188,14 +182,6 @@
     new_master = weights - step_size * scaled
     gathered[a, y, c, x] = new_master.astype(jnp.bfloat16)
 
-    stores = []
-
-    def store(where, slot):
-        copy = pltpu.make_async_copy(gathered.at[where], out_params.at[where], store_sem.at[slot])
-        copy.start()
-        stores.append(copy)
-
-    slots = iter(range(A * Y * S * X))
     own = (a, y, c, x)
     line_hops, plane_hops, core_hops = {}, {}, {}
     for d in lines_far:
@@ -221,34 +207,35 @@
     to_cores(0, len(plane), own)
     m_out[...] = new_master
     u_out[...] = scaled
-    for i, (src, dst) in enumerate(((m_out, out_master), (u_out, out_scaled))):
-        smalls.append(pltpu.make_async_copy(src, dst, small_sem.at[2 + i]))
-        smalls[-1].start()
-    store(own, next(slots))
     for d in lines_near:
         line_hops[d].wait_recv()
         block = at(d, 0, 0, 0, -1)
         to_plane(d)
         to_cores(d, len(plane), block)
-        store(block, next(slots))
     for d in [0] + lines_near:
         for i, (dy, dx) in enumerate(plane):
             plane_hops[d, i].wait_recv()
             block = at(d, dy, 0, dx, -1)
             to_cores(d, i, block)
-            store(block, next(slots))
     for d in [0] + lines_near:
         for i, (dy, dx) in [(len(plane), (0, 0))] + list(enumerate(plane)):
             for k in range(1, S):
                 core_hops[d, i, k].wait_recv()
-                store(at(d, dy, k, dx, -1), next(slots))
 
     for group in (pair, crossing, along, line_hops, plane_hops, core_hops):
         for copy in group.values():
             copy.wait_send()
     for copy in exchange:
         copy.wait_send()
-    for copy in stores + smalls:
+
+
+def write_out(*refs):
+    count = len(refs) // 2
+    sems = refs[-1]
+    copies = [pltpu.make_async_copy(refs[i], refs[count + i], sems.at[i]) for i in range(count)]
+    for copy in reversed(copies):
+        copy.start()
+    for copy in copies:
         copy.wait()
 
 
@@ -270,9 +257,9 @@
         small = jax.ShapeDtypeStruct((rows, width), f32)
         outs = pl.pallas_call(
             functools.partial(kernel, (A, Y, S, X)),
-            out_shape=(small, small, small, small, jax.ShapeDtypeStruct((A, Y, S, X, rows, width), bf16)),
+            out_shape=(vmem((rows, width), f32),) * 4 + (vmem((A, Y, S, X, rows, width), bf16),),
             in_specs=[anywhere] * 4 + [pl.BlockSpec(memory_space=vmem)],
-            out_specs=(anywhere,) * 5,
+            out_specs=(pl.BlockSpec(memory_space=vmem),) * 5,
             scratch_shapes=[
                 vmem((A, Y, X, rows, width), bf16),
                 vmem((cores, A, Y, X, rows, width), bf16),
@@ -285,11 +272,8 @@
                 vmem((rows, width), f32),
                 vmem((rows, width), f32),
                 vmem((rows, width), f32),
-                vmem((rows, width), f32),
-                vmem((rows, width), f32),
                 vmem((1, 128), f32),
                 vmem((max(total - 1, 1), 1, 128), f32),
-                vmem((A, Y, S, X, rows, width), bf16),
                 dma((A,)), dma((cores, A)), dma((3,)),
                 dma((cores, A)), dma((cores, A)),
                 dma((A, planes)), dma((A, planes)),
@@ -298,7 +282,6 @@
                 dma((lines,)), dma((lines,)),
                 dma((A, planes)), dma((A, planes)),
                 dma((cores, A, planes + 1)), dma((cores, A, planes + 1)),
-                dma((total,)), dma((4,)),
             ],
             compiler_params=pltpu.CompilerParams(collective_id=0, has_side_effects=True),
         )(
@@ -308,7 +291,14 @@
             second_moment,
             tensor_ids[None, :],
         )
-        return (*outs[:4], outs[4].reshape(total * rows, width))
+        written = pl.pallas_call(
+            write_out,
+            out_shape=(small,) * 4 + (jax.ShapeDtypeStruct((A, Y, S, X, rows, width), bf16),),
+            in_specs=[pl.BlockSpec(memory_space=vmem)] * 5,
+            out_specs=(anywhere,) * 5,
+            scratch_shapes=[dma((5,))],
+        )(*(pltpu.with_memory_space_constraint(out, vmem) for out in outs))
+        return (*written[:4], written[4].reshape(total * rows, width))
 
     axes = ("gx", "gy", "gz")
     return jax.shard_map(

time: 39.1 us -> 33.4 us (0.85); the launches traced: 38.4 us -> 33.2 us
  local copies, waits for them, and re-layouts: 5.75 us -> 0 us
  Pallas kernels: 32 us -> 32.6 us
    unnamed x11 -> x0, local copies, waits for them, and re-layouts: 5.75 us -> none
    pallas_call x1 -> x2, Pallas kernels: 32 us -> 32.6 us  [the longest x1 31.6 us: on_device(): pl.pallas_call(functools.partial(kernel, (A, Y, S, X)), out_shape=(vmem((...]
where the time goes in v2:
time: 33.4 us; the launch traced here: 33.2 us
  Pallas kernels  32.6 us (98%)
  between operations  0.64 us (2%)
    pallas_call x1, Pallas kernels, on_device(): pl.pallas_call(functools.partial(kernel, (A, Y, S, X)), out_shape=(vmem((...  31.6 us
    pallas_call x1, Pallas kernels, on_device(): pl.pallas_call(write_out, out_shape=(small,) * 4 + (jax.ShapeDtypeStruct(...  0.98 us

profile of v2, /device:TPU:0, one launch (start us, length us, event | category | flops | bytes accessed | tf_op | source)
XLA Modules:
  0.0 33.2 jit_solution(11865808161334337930)
XLA Ops:
  0.6 31.6 %shard_map.92 = (f32[24,512]{1,0:T(8,128)S(1)}, f32[24,512]{1,0:T(8,128)S(1)}, f32[24,512]{1,0:T(8,128)S(1)}, f32[24,512]{1,0:T(8,128)S(1)}, bf16[4,2,2,2,24,512]{5,4,3,2,1,0:T(8,128)(2,1)S(1)}) custom-call(bf16[4,2,2,2,24,512]{5,4,3,2,1,0:T(8,128)(2,1)} %bitcast.3, f32[24,512]{1,0:T(8,128)} %master.1, f32[24,512]{1,0:T(8,128)} %first.1, f32[24,512]{1,0:T(8,128)} %second.1, ...), custom_call_target="tpu_custom_call" | custom-call | tf_op jit(solution)/shard_map/pallas_call | solution.py:258
  32.3 1.0 %shard_map.93 = (f32[24,512]{1,0:T(8,128)}, f32[24,512]{1,0:T(8,128)}, f32[24,512]{1,0:T(8,128)}, f32[24,512]{1,0:T(8,128)}, bf16[4,2,2,2,24,512]{5,4,3,2,1,0:T(8,128)(2,1)}) custom-call(f32[24,512]{1,0:T(8,128)S(1)} %get-tuple-element.15.refs_0_, f32[24,512]{1,0:T(8,128)S(1)} %get-tuple-element.16.refs_1_, f32[24,512]{1,0:T(8,128)S(1)} %get-tuple-element.17.refs_2_, ...), custom_call_target="tpu_custom_call" | custom-call | tf_op jit(solution)/shard_map/pallas_call | solution.py:294

commit v3 on v2

--- a/solution.py
+++ b/solution.py
@@ -10,6 +10,8 @@
 
 NT = 4
 MESH = pl.DeviceIdType.MESH
+VMEM_BYTES = 67043328
+LARGEST_GRANT = 60 * 1024 * 1024
 
 decay_first = 0.9
 decay_second = 0.999
@@ -44,11 +46,12 @@
 
 def kernel(
     sizes, grads, master, first, second, ids,
-    m_out, first_out, second_out, u_out, gathered,
+    m_out, first_out, second_out, u_out, all_master, all_update, totals_out,
     own_half, far_half, pair_recv, pair_send, plane_recv, line_send, line_recv, acc,
-    m_in, f_in, s_in, sums_send, sums_recv,
+    m_in, f_in, s_in, line_sums, plane_sums, core_sums,
     load_own, load_far, load_small, pair_ss, pair_rs, plane_ss, plane_rs, line_ss, line_rs,
-    sums_ss, sums_rs, gl_ss, gl_rs, gp_ss, gp_rs, gs_ss, gs_rs,
+    sl_ss, sl_rs, sp_ss, sp_rs, sc_ss, sc_rs,
+    ml_ss, ml_rs, mp_ss, mp_rs, mc_ss, mc_rs, ul_ss, ul_rs, up_ss, up_rs, uc_ss, uc_rs,
 ):
     A, Y, S, X = sizes
     rows, width = master.shape
@@ -68,7 +71,7 @@
     plane = [q for q in itertools.product(range(Y), range(X)) if q != (0, 0)]
     lines_far = list(range(A - 1, 0, -1))
     lines_near = list(range(1, A))
-    others = [o for o in itertools.product(range(A), range(Y), range(S), range(X)) if o != (0, 0, 0, 0)]
+    others = [(d, 0, 0, 0) for d in lines_far] + [(0, dy, 0, dx) for dy, dx in plane] + [(0, 0, k, 0) for k in range(1, S)]
 
     def at(da, dy, dc, dx, sign=1):
         return (offset(a, da, A, sign), offset(y, dy, Y, sign), offset(c, dc, S, sign), offset(x, dx, X, sign))
@@ -99,7 +102,52 @@
 
     pl.semaphore_wait(barrier, len(others))
 
-    sends = []
+    own = (a, y, c, x)
+
+    class Gather:
+        def __init__(self, ref, line_sems, plane_sems, core_sems):
+            self.ref, self.line_sems, self.plane_sems, self.core_sems = ref, line_sems, plane_sems, core_sems
+            self.line, self.plane, self.core = {}, {}, {}
+
+        def copy(self, block, sems, slot, where):
+            ref = self.ref.at[block]
+            hop = remote(ref, ref, sems[0].at[slot], sems[1].at[slot], at(*where))
+            hop.start()
+            return hop
+
+        def to_line(self):
+            for d in lines_far:
+                self.line[d] = self.copy(own, self.line_sems, d - 1, (d, 0, 0, 0))
+
+        def to_plane(self, d):
+            for i, (dy, dx) in enumerate(plane):
+                self.plane[d, i] = self.copy(at(d, 0, 0, 0, -1), self.plane_sems, (d, i), (0, dy, 0, dx))
+
+        def to_core(self, d, i):
+            dy, dx = plane[i] if i < len(plane) else (0, 0)
+            for k in range(1, S):
+                self.core[d, i, k] = self.copy(at(d, dy, 0, dx, -1), self.core_sems, (k - 1, d, i), (0, 0, k, 0))
+
+        def relay_line(self, d):
+            self.line[d].wait_recv()
+            self.to_plane(d)
+            self.to_core(d, len(plane))
+
+        def relay_plane(self, d):
+            for i in range(len(plane)):
+                self.plane[d, i].wait_recv()
+                self.to_core(d, i)
+
+        def finish(self):
+            for hop in self.core.values():
+                hop.wait_recv()
+            for group in (self.line, self.plane, self.core):
+                for hop in group.values():
+                    hop.wait_send()
+
+    of_master = Gather(all_master, (ml_ss, ml_rs), (mp_ss, mp_rs), (mc_ss, mc_rs))
+    of_update = Gather(all_update, (ul_ss, ul_rs), (up_ss, up_rs), (uc_ss, uc_rs))
+
     pair = {}
     for d in order:
         for k in range(1, S):
@@ -117,6 +165,10 @@
     for copy in loads_small:
         copy.wait()
     weights = m_in[...]
+    all_master[own] = weights.astype(jnp.bfloat16)
+    of_master.to_line()
+    of_master.to_plane(0)
+    of_master.to_core(0, len(plane))
     weight_rows = jnp.sum(weights * weights, axis=1, keepdims=True)
     fixed_sums = jnp.where(hit_w, weight_rows, 0.0) + jnp.where(hit_n, float(width), 0.0)
 
@@ -142,6 +194,9 @@
 
     along = {}
     for d in order:
+        if d == 0:
+            for near in lines_near:
+                of_master.relay_line(near)
         total = acc[d]
         for i in range(len(plane)):
             crossing[d, i].wait_recv()
@@ -162,79 +217,100 @@
     update = new_first / (jnp.sqrt(new_second) + epsilon) + weight_decay * weights
     update_rows = jnp.sum(update * update, axis=1, keepdims=True)
     own_sums = jnp.sum(fixed_sums + jnp.where(hit_u, update_rows, 0.0), axis=0, keepdims=True)
-    sums_send[...] = own_sums
-    exchange = []
-    for i, o in enumerate(reversed(others)):
-        exchange.append(remote(sums_send, sums_recv.at[i], sums_ss.at[i], sums_rs.at[i], at(*o)))
-        exchange[-1].start()
+    line_sums[a] = own_sums
+    hops = []
+
+    def send_sums(ref, mine, sems, slot, where):
+        hops.append(remote(ref.at[mine], ref.at[mine], sems[0].at[slot], sems[1].at[slot], at(*where)))
+        hops[-1].start()
+        return hops[-1]
+
+    sums_line = [send_sums(line_sums, a, (sl_ss, sl_rs), d - 1, (d, 0, 0, 0)) for d in lines_far]
+    all_update[own] = update.astype(jnp.bfloat16)
+    of_update.to_line()
+    of_update.to_plane(0)
+    of_update.to_core(0, len(plane))
     first_out[...] = new_first
     second_out[...] = new_second
-    totals = own_sums
-    for i in reversed(range(len(others))):
-        exchange[i].wait_recv()
-        totals = totals + sums_recv[i]
+    for d in [0] + lines_near:
+        of_master.relay_plane(d)
+    for d in lines_near[:-1]:
+        of_update.relay_line(d)
+    for hop in sums_line:
+        hop.wait_recv()
+    subtotal = line_sums[0]
+    for i in range(1, A):
+        subtotal = subtotal + line_sums[i]
+    here = y * X + x
+    plane_sums[here] = subtotal
+    sums_plane = [
+        send_sums(plane_sums, here, (sp_ss, sp_rs), i, (0, dy, 0, dx)) for i, (dy, dx) in enumerate(plane)
+    ]
+    for d in lines_near[-1:]:
+        of_update.relay_line(d)
+    of_update.relay_plane(0)
+    for hop in sums_plane:
+        hop.wait_recv()
+    subtotal = plane_sums[0]
+    for i in range(1, Y * X):
+        subtotal = subtotal + plane_sums[i]
+    core_sums[c] = subtotal
+    sums_core = [send_sums(core_sums, c, (sc_ss, sc_rs), k - 1, (0, 0, k, 0)) for k in range(1, S)]
+    for d in lines_near[:-1]:
+        of_update.relay_plane(d)
+    for hop in sums_core:
+        hop.wait_recv()
+    totals = core_sums[0]
+    for i in range(1, S):
+        totals = totals + core_sums[i]
+    totals_out[...] = totals
     row_totals = jnp.broadcast_to(totals, (rows, 128))
     row_weight, row_update, row_count = (
         jnp.sum(jnp.where(hit, row_totals, 0.0), axis=1, keepdims=True) for hit in (hit_w, hit_u, hit_n)
     )
     trust = jnp.sqrt(row_weight / (row_update + row_count))
     scaled = trust * update
-    new_master = weights - step_size * scaled
-    gathered[a, y, c, x] = new_master.astype(jnp.bfloat16)
-
-    own = (a, y, c, x)
-    line_hops, plane_hops, core_hops = {}, {}, {}
-    for d in lines_far:
-        line_hops[d] = remote(gathered.at[own], gathered.at[own], gl_ss.at[d - 1], gl_rs.at[d - 1], at(d, 0, 0, 0))
-        line_hops[d].start()
-
-    def to_plane(d):
-        block = at(d, 0, 0, 0, -1)
-        for i, (dy, dx) in enumerate(plane):
-            plane_hops[d, i] = remote(
-                gathered.at[block], gathered.at[block], gp_ss.at[d, i], gp_rs.at[d, i], at(0, dy, 0, dx)
-            )
-            plane_hops[d, i].start()
-
-    def to_cores(d, i, block):
-        for k in range(1, S):
-            core_hops[d, i, k] = remote(
-                gathered.at[block], gathered.at[block], gs_ss.at[k - 1, d, i], gs_rs.at[k - 1, d, i], at(0, 0, k, 0)
-            )
-            core_hops[d, i, k].start()
-
-    to_plane(0)
-    to_cores(0, len(plane), own)
-    m_out[...] = new_master
+    m_out[...] = weights - step_size * scaled
     u_out[...] = scaled
-    for d in lines_near:
-        line_hops[d].wait_recv()
-        block = at(d, 0, 0, 0, -1)
-        to_plane(d)
-        to_cores(d, len(plane), block)
-    for d in [0] + lines_near:
-        for i, (dy, dx) in enumerate(plane):
-            plane_hops[d, i].wait_recv()
-            block = at(d, dy, 0, dx, -1)
-            to_cores(d, i, block)
-    for d in [0] + lines_near:
-        for i, (dy, dx) in [(len(plane), (0, 0))] + list(enumerate(plane)):
-            for k in range(1, S):
-                core_hops[d, i, k].wait_recv()
-
-    for group in (pair, crossing, along, line_hops, plane_hops, core_hops):
+    for d in lines_near[-1:]:
+        of_update.relay_plane(d)
+    of_master.finish()
+    of_update.finish()
+    for group in (pair, crossing, along):
         for copy in group.values():
             copy.wait_send()
-    for copy in exchange:
-        copy.wait_send()
-
-
-def write_out(*refs):
-    count = len(refs) // 2
-    sems = refs[-1]
-    copies = [pltpu.make_async_copy(refs[i], refs[count + i], sems.at[i]) for i in range(count)]
-    for copy in reversed(copies):
+    for hop in hops:
+        hop.wait_send()
+
+
+def write_out(sizes, all_master, all_update, totals, *refs):
+    A, Y, S, X = sizes
+    rows, width = all_master.shape[-2:]
+    kept, out_kept, out_params, params, sems, param_sems = refs[:4], refs[4:8], refs[8], refs[9], refs[10], refs[11]
+    copies = [pltpu.make_async_copy(kept[i], out_kept[i], sems.at[i]) for i in range(4)]
+    for copy in copies:
         copy.start()
+    values = totals[...]
+    weight_sq, update_sq, counts = (
+        [values[:, group * NT + t : group * NT + t + 1] for t in range(NT)] for group in range(3)
+    )
+    steps = [step_size * jnp.sqrt(weight_sq[t] / (update_sq[t] + counts[t])) for t in range(NT)]
+    ends, end = [], 0.0
+    for t in range(NT - 1):
+        end = end + counts[t]
+        ends.append(end)
+    row_of = lax.broadcasted_iota(jnp.int32, (rows, 1), 0)
+    for i in range(A):
+        for j, (y, c, x) in enumerate(itertools.product(range(Y), range(S), range(X))):
+            block = i * Y * S * X + j
+            place = ((row_of + block * rows) * width).astype(jnp.float32)
+            step = jnp.broadcast_to(steps[NT - 1], (rows, 1))
+            for t in reversed(range(NT - 1)):
+                step = jnp.where(place < ends[t], steps[t], step)
+            value = all_master[i, y, c, x].astype(jnp.float32) - step * all_update[i, y, c, x].astype(jnp.float32)
+            params[i, y, c, x] = value.astype(jnp.bfloat16)
+        copies.append(pltpu.make_async_copy(params.at[i], out_params.at[i], param_sems.at[i]))
+        copies[-1].start()
     for copy in copies:
         copy.wait()
 
@@ -255,11 +331,13 @@
         anywhere = pl.BlockSpec(memory_space=pl.ANY)
         vmem = pltpu.VMEM
         small = jax.ShapeDtypeStruct((rows, width), f32)
+        kept_bytes = rows * width * 4 * (total + 4) + 1024 * 1024
+        grant = min(LARGEST_GRANT, VMEM_BYTES - kept_bytes)
         outs = pl.pallas_call(
             functools.partial(kernel, (A, Y, S, X)),
-            out_shape=(vmem((rows, width), f32),) * 4 + (vmem((A, Y, S, X, rows, width), bf16),),
+            out_shape=(vmem((rows, width), f32),) * 4 + (vmem((A, Y, S, X, rows, width), bf16),) * 2 + (vmem((1, 128), f32),),
             in_specs=[anywhere] * 4 + [pl.BlockSpec(memory_space=vmem)],
-            out_specs=(pl.BlockSpec(memory_space=vmem),) * 5,
+            out_specs=(pl.BlockSpec(memory_space=vmem),) * 7,
             scratch_shapes=[
                 vmem((A, Y, X, rows, width), bf16),
                 vmem((cores, A, Y, X, rows, width), bf16),
@@ -272,18 +350,20 @@
                 vmem((rows, width), f32),
                 vmem((rows, width), f32),
                 vmem((rows, width), f32),
-                vmem((1, 128), f32),
-                vmem((max(total - 1, 1), 1, 128), f32),
+                vmem((A, 1, 128), f32),
+                vmem((Y * X, 1, 128), f32),
+                vmem((S, 1, 128), f32),
                 dma((A,)), dma((cores, A)), dma((3,)),
                 dma((cores, A)), dma((cores, A)),
                 dma((A, planes)), dma((A, planes)),
                 dma((lines,)), dma((lines,)),
-                dma((total,)), dma((total,)),
-                dma((lines,)), dma((lines,)),
-                dma((A, planes)), dma((A, planes)),
+                dma((lines,)), dma((lines,)), dma((planes,)), dma((planes,)), dma((cores,)), dma((cores,)),
+                dma((lines,)), dma((lines,)), dma((A, planes)), dma((A, planes)),
+                dma((cores, A, planes + 1)), dma((cores, A, planes + 1)),
+                dma((lines,)), dma((lines,)), dma((A, planes)), dma((A, planes)),
                 dma((cores, A, planes + 1)), dma((cores, A, planes + 1)),
             ],
-            compiler_params=pltpu.CompilerParams(collective_id=0, has_side_effects=True),
+            compiler_params=pltpu.CompilerParams(collective_id=0, has_side_effects=True, vmem_limit_bytes=grant),
         )(
             gradients.reshape(A, Y, S, X, rows, width),
             master_weights,
@@ -291,13 +371,15 @@
             second_moment,
             tensor_ids[None, :],
         )
+        outs = [pltpu.with_memory_space_constraint(out, vmem) for out in outs]
         written = pl.pallas_call(
-            write_out,
+            functools.partial(write_out, (A, Y, S, X)),
             out_shape=(small,) * 4 + (jax.ShapeDtypeStruct((A, Y, S, X, rows, width), bf16),),
-            in_specs=[pl.BlockSpec(memory_space=vmem)] * 5,
+            in_specs=[pl.BlockSpec(memory_space=vmem)] * 7,
             out_specs=(anywhere,) * 5,
-            scratch_shapes=[dma((5,))],
-        )(*(pltpu.with_memory_space_constraint(out, vmem) for out in outs))
+            scratch_shapes=[vmem((A, Y, S, X, rows, width), bf16), dma((4,)), dma((A,))],
+            compiler_params=pltpu.CompilerParams(vmem_limit_bytes=grant),
+        )(outs[4], outs[5], outs[6], outs[0], outs[1], outs[2], outs[3])
         return (*written[:4], written[4].reshape(total * rows, width))
 
     axes = ("gx", "gy", "gz")

time: 33.4 us -> 29.7 us (0.89)
  Pallas kernels: 32.6 us -> 28.9 us
    pallas_call x1, Pallas kernels: 31.6 us -> 27.6 us  [on_device(): pl.pallas_call(functools.partial(kernel, (A, Y, S, X)), out_shape=(vmem((...]
    pallas_call x1, Pallas kernels: 0.98 us -> 1.37 us  [on_device(): pl.pallas_call(functools.partial(write_out, (A, Y, S, X)), out_shape=(sma...]
where the time goes in v3:
time: 29.7 us; the launch traced here: 29.6 us
  Pallas kernels  28.9 us (97%)
  between operations  0.64 us (2%)
    pallas_call x1, Pallas kernels, on_device(): pl.pallas_call(functools.partial(kernel, (A, Y, S, X)), out_shape=(vmem((...  27.6 us
    pallas_call x1, Pallas kernels, on_device(): pl.pallas_call(functools.partial(write_out, (A, Y, S, X)), out_shape=(sma...  1.37 us

profile of v3, /device:TPU:0, one launch (start us, length us, event | category | flops | bytes accessed | tf_op | source)
XLA Modules:
  0.0 29.6 jit_solution(6396487460699745613)
XLA Ops:
  0.6 27.6 %shard_map.92 = (f32[24,512]{1,0:T(8,128)S(1)}, f32[24,512]{1,0:T(8,128)S(1)}, f32[24,512]{1,0:T(8,128)S(1)}, f32[24,512]{1,0:T(8,128)S(1)}, bf16[4,2,2,2,24,512...) custom-call(bf16[4,2,2,2,24,512]{5,4,3,2,1,0:T(8,128)(2,1)} %bitcast.3, ...), custom_call_target="tpu_custom_call" | custom-call | tf_op jit(solution)/shard_map/pallas_call | solution.py:336
  28.2 1.4 %shard_map.93 = (f32[24,512]{1,0:T(8,128)}, f32[24,512]{1,0:T(8,128)}, f32[24,512]{1,0:T(8,128)}, f32[24,512]{1,0:T(8,128)}, bf16[4,2,2,2,24,512]{5,4,3,2,1,0:T(8,128)(2,1)}) custom-call(bf16[4,2,2,2,24,512]{5,4,3,2,1,0:T(8,128)(2,1)S(1)} %get-tuple-element.17.all_master, bf16[4,2,2,2,24,512]{5,4,3,2,1,0:T(8,128)(2,1)S(1)} %get-tuple-element.18.all_update, ...), custom_call_target="tpu_custom_call" | custom-call | tf_op jit(solution)/shard_map/pallas_call | solution.py:375

commit v4 on v3

--- a/solution.py
+++ b/solution.py
@@ -232,8 +232,7 @@
     of_update.to_core(0, len(plane))
     first_out[...] = new_first
     second_out[...] = new_second
-    for d in [0] + lines_near:
-        of_master.relay_plane(d)
+    of_master.relay_plane(0)
     for d in lines_near[:-1]:
         of_update.relay_line(d)
     for hop in sums_line:
@@ -248,6 +247,8 @@
     ]
     for d in lines_near[-1:]:
         of_update.relay_line(d)
+    for d in lines_near:
+        of_master.relay_plane(d)
     of_update.relay_plane(0)
     for hop in sums_plane:
         hop.wait_recv()

time: 29.7 us -> 29.6 us (level)
  no operation moved by 1% of the time
where the time goes in v4:
time: 29.6 us; the launch traced here: 29.5 us
  Pallas kernels  28.8 us (97%)
  between operations  0.64 us (2%)
    pallas_call x1, Pallas kernels, on_device(): pl.pallas_call(functools.partial(kernel, (A, Y, S, X)), out_shape=(vmem((...  27.5 us
    pallas_call x1, Pallas kernels, on_device(): pl.pallas_call(functools.partial(write_out, (A, Y, S, X)), out_shape=(sma...  1.37 us

profile of v4, /device:TPU:0, one launch (start us, length us, event | category | flops | bytes accessed | tf_op | source)
XLA Modules:
  0.0 29.5 jit_solution(11926207900569730219)
XLA Ops:
  0.6 27.5 %shard_map.92 = (f32[24,512]{1,0:T(8,128)S(1)}, f32[24,512]{1,0:T(8,128)S(1)}, f32[24,512]{1,0:T(8,128)S(1)}, f32[24,512]{1,0:T(8,128)S(1)}, bf16[4,2,2,2,24,512...) custom-call(bf16[4,2,2,2,24,512]{5,4,3,2,1,0:T(8,128)(2,1)} %bitcast.3, ...), custom_call_target="tpu_custom_call" | custom-call | tf_op jit(solution)/shard_map/pallas_call | solution.py:337
  28.1 1.4 %shard_map.93 = (f32[24,512]{1,0:T(8,128)}, f32[24,512]{1,0:T(8,128)}, f32[24,512]{1,0:T(8,128)}, f32[24,512]{1,0:T(8,128)}, bf16[4,2,2,2,24,512]{5,4,3,2,1,0:T(8,128)(2,1)}) custom-call(bf16[4,2,2,2,24,512]{5,4,3,2,1,0:T(8,128)(2,1)S(1)} %get-tuple-element.17.all_master, bf16[4,2,2,2,24,512]{5,4,3,2,1,0:T(8,128)(2,1)S(1)} %get-tuple-element.18.all_update, ...), custom_call_target="tpu_custom_call" | custom-call | tf_op jit(solution)/shard_map/pallas_call | solution.py:376
